TPU v7x, 32 devices: a whole 2x2x4 slice. The times are simulated.
32 devices in a mesh: rep: 2 (over y), ep: 16 (over z, x, core).
Axes of the slice: x: 2, y: 2, z: 4, core: 2. Of those that a mesh axis runs over, the one named last changes fastest.
Arguments:
- cache_kv: bfloat16 [64, 2048, 576], P(('rep', 'ep')), parts along dimension 0, may hold values from -6 to 6
- new_kv: bfloat16 [64, 2, 576], P(('rep', 'ep')), parts along dimension 0, may hold values from -6 to 6
- queries: bfloat16 [64, 2, 64, 576], P(('rep', 'ep')), parts along dimension 0, may hold values from -256 to 256
- lengths: int32 [64], P(('rep', 'ep')), parts along dimension 0, may hold values from 256 to 2048
- resid: bfloat16 [64, 2, 7168], P(('rep', 'ep')), parts along dimension 0, may hold values from -18 to 18
- value_up: bfloat16 [512, 8192], P(None, 'ep'), may hold values from -1.5 to 1.5
- out_proj: bfloat16 [8192, 7168], P('ep'), may hold values from -0.09375 to 0.09375
- norm_gain: bfloat16 [7168], replicated, may hold values from 0.25 to 1.75
- router: bfloat16 [7168, 16], replicated, may hold values from -0.0625 to 0.0625
- expert_ids: int32 [64, 2, 8], P(('rep', 'ep')), parts along dimension 0, may hold values from 0 to 15, as said below
- slots: int32 [64, 2, 8], P(('rep', 'ep')), parts along dimension 0, may hold values from 0 to 3, as said below
- w_gate: bfloat16 [7168, 16384], P(None, 'ep'), may hold values from -0.0625 to 0.0625
- w_up: bfloat16 [7168, 16384], P(None, 'ep'), may hold values from -0.0625 to 0.0625
- w_down: bfloat16 [16384, 7168], P('ep'), may hold values from -0.1875 to 0.1875
Outputs:
- mixed: bfloat16 [64, 2, 7168], P(('rep', 'ep')), parts along dimension 0
There are 2 independent parts, one for each index of `rep`. A program takes and returns all parts, laid end to end along the dimension named above; an argument that names none is the same for every part. Nothing has to cross between parts.
Inputs may be any that keep to these rules, and one draw needn't show every extreme that they name: `expert_ids`: each row names 8 different experts. In each aligned block of 4 rows (the rows of one device), the rows that name the same expert carry the distinct slots 0 up to their number minus one for it; in every block some expert is named by all 4 rows.
All inputs are finite; a program needn't handle non-finite values.
Results may differ from a plain program's by a relative error of at most 0.0065.
Values may be sent and summed in bfloat16 or wider, within the bound.
A program may use at most 128 MiB of HBM per device.

v0:
```python
import math

import jax
import jax.numpy as jnp
from jax import lax
from jax.sharding import PartitionSpec as P

D = 7168
H = 64
LAT = 512
VH = 128
EXPERTS = 16
TOP = 8
CAP = 2
QK = 192


route_scale = 2.827
norm_eps = 1e-06


def softmax_parts(score_cache, score_new):
    row_peak = jnp.maximum(jnp.max(score_cache, axis=-1), jnp.max(score_new, axis=-1))
    exp_cache = jnp.exp(score_cache - row_peak[..., None])
    exp_new = jnp.exp(score_new - row_peak[..., None])
    exp_total = jnp.sum(exp_cache, axis=-1) + jnp.sum(exp_new, axis=-1)
    prob_cache = (exp_cache / exp_total[..., None]).astype(jnp.bfloat16)
    prob_new = (exp_new / exp_total[..., None]).astype(jnp.bfloat16)
    return (prob_cache, prob_new)


def attention(cache_kv, new_kv, queries, lengths):
    score_scale = 1.0 / math.sqrt(QK)
    cache_len = cache_kv.shape[1]
    step_count = new_kv.shape[1]
    score_new = (
        jnp.einsum("bshk,btk->bsht", queries, new_kv, preferred_element_type=jnp.float32)
        * score_scale
    )
    step_ids = jnp.arange(step_count, dtype=jnp.int32)
    causal = step_ids[None, :] <= step_ids[:, None]
    score_new = jnp.where(causal[None, :, None, :], score_new, -jnp.inf)
    score_cache = (
        jnp.einsum("bshk,bpk->bshp", queries, cache_kv, preferred_element_type=jnp.float32)
        * score_scale
    )
    position = jnp.arange(cache_len, dtype=jnp.int32)
    is_live = position[None, :] < lengths[:, None]
    score_cache = jnp.where(is_live[:, None, None, :], score_cache, -jnp.inf)
    prob_cache, prob_new = softmax_parts(score_cache, score_new)
    context = jnp.einsum(
        "bshp,bpc->bshc", prob_cache, cache_kv[:, :, :LAT], preferred_element_type=jnp.float32
    )
    context = context + jnp.einsum(
        "bsht,btc->bshc", prob_new, new_kv[:, :, :LAT], preferred_element_type=jnp.float32
    )
    return context.astype(jnp.bfloat16)


def expert_ffn(token_rows, w_gate, w_up, w_down):
    gate = jnp.dot(token_rows, w_gate, preferred_element_type=jnp.float32)
    upward = jnp.dot(token_rows, w_up, preferred_element_type=jnp.float32)
    act = (jax.nn.silu(gate) * upward).astype(jnp.bfloat16)
    return jnp.dot(act, w_down, preferred_element_type=jnp.float32)


def route_weights(token_rows, route_ids, router):
    logits = jnp.dot(token_rows, router, preferred_element_type=jnp.float32)
    expert_range = jnp.arange(router.shape[1], dtype=jnp.int32)
    is_pick = route_ids[:, :, None] == expert_range[None, None, :]
    picked = jnp.sum(jnp.where(is_pick, logits[:, None, :], 0.0), axis=-1)
    gates = jax.nn.sigmoid(picked)
    return route_scale * gates / jnp.sum(gates, axis=1, keepdims=True)


def body(
    cache_kv,
    new_kv,
    queries,
    lengths,
    resid,
    value_up,
    out_proj,
    norm_gain,
    router,
    expert_ids,
    slots,
    w_gate,
    w_up,
    w_down,
):
    devices = lax.axis_size("ep")
    context = attention(cache_kv, new_kv, queries, lengths)
    tok_count = context.shape[0] * context.shape[1]
    context = context.reshape(tok_count, H, LAT)
    value_cols = value_up.shape[1]
    heads_per = max(1, value_cols // VH)
    if value_cols < VH:
        outgoing = jnp.repeat(context, VH // value_cols, axis=1)
    else:
        outgoing = context
    outgoing = outgoing.reshape(tok_count, devices, heads_per * LAT)
    arrived = lax.all_to_all(outgoing, "ep", split_axis=1, concat_axis=0, tiled=True)
    head_rows = arrived.reshape(devices * tok_count, heads_per, LAT)
    value_table = value_up.reshape(LAT, heads_per, value_cols // heads_per)
    values = jnp.einsum("rhc,chv->rhv", head_rows, value_table, preferred_element_type=jnp.float32)
    values = values.astype(jnp.bfloat16).reshape(devices * tok_count, value_cols)
    attended = lax.psum_scatter(
        jnp.dot(values, out_proj, preferred_element_type=jnp.float32),
        "ep",
        scatter_dimension=0,
        tiled=True,
    )
    hidden = resid.reshape(tok_count, D).astype(jnp.float32) + attended
    mean_square = jnp.mean(hidden * hidden, axis=-1, keepdims=True)
    normed = (hidden * lax.rsqrt(mean_square + norm_eps) * norm_gain.astype(jnp.float32)).astype(
        jnp.bfloat16
    )
    route_ids = expert_ids.reshape(tok_count, TOP)
    route_slots = slots.reshape(tok_count, TOP)
    group_size = devices // EXPERTS
    weights = route_weights(normed, route_ids, router)
    expert_grid = (
        route_ids[:, :, None] == jnp.arange(EXPERTS, dtype=jnp.int32)[None, None, :]
    ).astype(jnp.float32)
    slot_grid = (route_slots[:, :, None] == jnp.arange(CAP, dtype=jnp.int32)[None, None, :]).astype(
        jnp.float32
    )
    places = jnp.sum(expert_grid[:, :, :, None] * slot_grid[:, :, None, :], axis=1)
    shares = jnp.sum(
        expert_grid[:, :, :, None] * slot_grid[:, :, None, :] * weights[:, :, None, None], axis=1
    )
    places_dest = jnp.repeat(places, group_size, axis=1)
    shares_dest = jnp.repeat(shares, group_size, axis=1)
    outgoing_rows = jnp.einsum(
        "tjc,td->jcd", places_dest.astype(jnp.bfloat16), normed, preferred_element_type=jnp.float32
    ).astype(jnp.bfloat16)
    slot_rows = lax.all_to_all(outgoing_rows, "ep", split_axis=0, concat_axis=0, tiled=True)
    flat_rows = slot_rows.reshape(-1, slot_rows.shape[2])
    produced = expert_ffn(flat_rows, w_gate, w_up, w_down)
    produced = produced.reshape(slot_rows.shape[0], slot_rows.shape[1], produced.shape[1])
    returned = lax.all_to_all(
        produced.astype(jnp.bfloat16), "ep", split_axis=0, concat_axis=0, tiled=True
    ).astype(produced.dtype)
    expert_mix = jnp.dot(
        shares_dest.reshape(tok_count, devices * CAP),
        returned.reshape(devices * CAP, D),
        precision=lax.Precision.HIGHEST,
    )
    mixed = (hidden + expert_mix).astype(jnp.bfloat16)
    return mixed.reshape(resid.shape)


def solution(mesh):
    return jax.shard_map(
        body,
        mesh=mesh,
        in_specs=(
            P(("rep", "ep"), None, None),
            P(("rep", "ep"), None, None),
            P(("rep", "ep"), None, None, None),
            P(("rep", "ep")),
            P(("rep", "ep"), None, None),
            P(None, "ep"),
            P("ep", None),
            P(),
            P(),
            P(("rep", "ep"), None, None),
            P(("rep", "ep"), None, None),
            P(None, "ep"),
            P(None, "ep"),
            P("ep", None),
        ),
        out_specs=P(("rep", "ep"), None, None),
        check_vma=False,
    )
```

profile of v0, /device:TPU:0, one launch (start us, length us, event | category | flops | bytes accessed | tf_op | source)
XLA Modules:
  0.0 200.3 jit_solution(1113551979265090993)
XLA Ops:
  6.5 0.0 copy-start
  6.5 0.0 all-reduce.3.cloned.1.call-start
  6.5 0.8 iota_compare_fusion.1
  7.3 0.0 copy-start.3
  7.4 0.0 copy-start.7
  7.4 0.0 copy-start.2
  7.4 3.8 %fusion.46 = (f32[2,2,64]{2,1,0:T(2,128)S(1)}, f32[2,2,64,2048]{3,2,1,0:T(8,128)S(1)}) fusion(bf16[2,2,64,576]{3,2,1,0:T(8,128)(2,1)} %param.16, bf16[2,2048,576]{1,2,0:T(8,128)(2,1)} %param.14, pred[2,2048]{1,0:T(4,128)(4,1)S(1)} %iota_compare_fusion.1), kind=kOutput, calls=%fused_computation.66 | convolution fusion | flops 605552384 | bytes 7115776 | tf_op jit(solution)/shard_map/bshk,bpk->bshp/dot_general | solution.py:44
  11.1 0.0 copy-done.3
  11.2 0.0 copy-done.7
  11.2 0.3 fusion.47
  11.5 0.4 fusion.13
  11.9 0.0 copy-done.2
  11.9 1.7 fusion.4
  13.7 0.3 fusion.14
  14.0 0.2 reshape_reshape.3
  14.1 0.2 copy.33
  14.3 17.2 %all_to_all.25 = bf16[4,16,2048]{2,0,1:T(4,128)(2,1)S(1)} all-to-all(bf16[4,16,2048]{2,0,1:T(4,128)(2,1)S(1)} %copy.33), channel_id=1, replica_groups=mesh['rep'=2,'ep'=16] {'ep'}, dimensions={1} | all-to-all | bytes 524288 | tf_op jit(solution)/shard_map/all_to_all | solution.py:103
  31.5 0.2 reshape.104
  31.7 0.0 copy-done
  31.7 0.2 fusion.16
  32.0 0.0 copy-start.4
  32.0 0.0 copy-start.5
  32.0 0.0 copy-start.10
  32.0 0.0 copy-start.8
  32.0 0.0 copy-start.6
  32.0 0.0 copy-start.9
  32.0 5.8 %fusion.29 = f32[64,7168]{1,0:T(8,128)} fusion(bf16[512,7168]{1,0:T(8,128)(2,1)} %param.20, bf16[4,8,8,128]{3,2,1,0:T(8,128)(2,1)S(1)} %fusion.16), kind=kOutput, calls=%fused_computation.37 | convolution fusion | flops 469762048 | bytes 9240576 | tf_op jit(solution)/shard_map/dot_general | solution.py:109
  37.8 0.0 all-reduce.3.cloned.1.call-update
  37.8 0.0 copy-done.4
  37.9 0.0 copy-done.5
  37.9 0.0 copy-done.10
  37.9 0.6 dynamic-slice
  39.2 0.0 copy-done.8
  39.2 0.0 copy-done.6
  39.2 0.1 fusion.35
  39.3 94.1 %all-reduce.3.cloned.1.call-done = f32[64,7168]{1,0:T(8,128)} async-done(((f32[64,7168]{1,0:T(8,128)}), f32[64,7168]{1,0:T(8,128)}) %all-reduce.3.cloned.1.call-update) | async-done | bytes 1835024
  133.4 1.1 multiply_reduce_fusion
  134.5 0.1 multiply_convert_fusion
  134.6 0.0 copy-done.9
  134.6 0.2 fusion.48
  134.8 0.2 select_reduce_fusion
  134.9 0.1 fusion.45
  135.1 0.1 multiply_divide_fusion
  135.1 0.1 fusion.34
  135.3 0.3 convolution_convert_fusion.1
  135.6 0.5 copy.38
  136.1 16.8 %all_to_all.26 = bf16[16,2,7168]{2,1,0:T(2,128)(2,1)S(1)} all-to-all(bf16[16,2,7168]{2,1,0:T(2,128)(2,1)S(1)} %copy.38), channel_id=1, replica_groups=mesh['rep'=2,'ep'=16] {'ep'}, dimensions={0} | all-to-all | bytes 917504 | tf_op jit(solution)/shard_map/all_to_all | solution.py:138
  152.9 0.2 reshape.107
  153.0 7.8 %fusion.49 = f32[32,1024]{1,0:T(8,128)S(1)} fusion(bf16[32,7168]{1,0:T(8,128)(2,1)S(1)} %reshape.107, bf16[7168,1024]{1,0:T(8,128)(2,1)} %param.25), kind=kOutput, calls=%fused_computation.69 | convolution fusion | flops 469762048 | bytes 15269888 | tf_op jit(solution)/shard_map/dot_general | solution.py:61
  160.8 0.0 copy-start.1
  160.8 14.6 %convolution_convert_fusion = bf16[32,7168]{1,0:T(8,128)(2,1)S(1)} fusion(bf16[1024,7168]{1,0:T(8,128)(2,1)} %param.27, bf16[32,7168]{1,0:T(8,128)(2,1)S(1)} %reshape.107, bf16[7168,1024]{1,0:T(8,128)(2,1)} %param.26, f32[32,1024]{1,0:T(8,128)S(1)} %fusion.49), kind=kOutput, calls=%fused_computation | convolution fusion | flops 939950080 | bytes 30408704 | tf_op jit(solution)/shard_map/dot_general | solution.py:64
  175.4 0.2 convert_element_type.75
  175.6 16.8 %all_to_all.27 = bf16[16,2,7168]{2,1,0:T(2,128)(2,1)S(1)} all-to-all(bf16[16,2,7168]{2,1,0:T(2,128)(2,1)S(1)} %convert_element_type.75), channel_id=1, replica_groups=mesh['rep'=2,'ep'=16] {'ep'}, dimensions={0} | all-to-all | bytes 917504 | tf_op jit(solution)/shard_map/all_to_all | solution.py:142
  192.4 0.4 fusion.1
  192.8 0.6 reshape.108
  193.5 0.0 copy-done.1
  (8 shorter events, 0.1 us)
Async XLA Ops:
  6.5 25.2 %copy-start = (bf16[512,512]{1,0:T(8,128)(2,1)S(1)}, bf16[512,512]{1,0:T(8,128)(2,1)}, u32[]{:S(2)}) copy-start(bf16[512,512]{1,0:T(8,128)(2,1)} %param.19) | copy-start | bytes 1572868
  6.5 126.8 %all-reduce.3.cloned.1.call-start = ((), (), s32[]{:S(2)}) async-start(), calls=%async_computation.3 | async-start | bytes 3670016
  7.3 3.8 %copy-start.3 = (bf16[2,2,64,576]{3,2,1,0:T(8,128)(2,1)S(1)}, bf16[2,2,64,576]{3,2,1,0:T(8,128)(2,1)}, u32[]{:S(2)}) copy-start(bf16[2,2,64,576]{3,2,1,0:T(8,128)(2,1)} %param.16) | copy-start | bytes 884740
  7.4 3.8 %copy-start.7 = (bf16[2,2,576]{2,1,0:T(2,128)(2,1)S(1)}, bf16[2,2,576]{2,1,0:T(2,128)(2,1)}, u32[]{:S(2)}) copy-start(bf16[2,2,576]{2,1,0:T(2,128)(2,1)} %param.15) | copy-start | bytes 13828
  7.4 4.6 %copy-start.2 = (bf16[2,2048,576]{1,2,0:T(8,128)(2,1)S(1)}, bf16[2,2048,576]{1,2,0:T(8,128)(2,1)}, u32[]{:S(2)}) copy-start(bf16[2,2048,576]{1,2,0:T(8,128)(2,1)} %param.14) | copy-start | bytes 14155780
  32.0 5.9 %copy-start.4 = (bf16[2,2,7168]{2,1,0:T(2,128)(2,1)S(1)}, bf16[2,2,7168]{2,1,0:T(2,128)(2,1)}, u32[]{:S(2)}) copy-start(bf16[2,2,7168]{2,1,0:T(2,128)(2,1)} %param.18) | copy-start | bytes 172036
  32.0 5.9 %copy-start.5 = (bf16[7168]{0:T(1024)(128)(2,1)S(1)}, bf16[7168]{0:T(1024)(128)(2,1)}, u32[]{:S(2)}) copy-start(bf16[7168]{0:T(1024)(128)(2,1)} %param.21) | copy-start | bytes 43012
  32.0 5.9 %copy-start.10 = (u32[32]{0:T(128)S(1)}, u32[32]{0:T(128)}, u32[]{:S(2)}) copy-start(u32[32]{0:T(128)} %constant.27) | copy-start | bytes 388
  32.0 7.2 %copy-start.8 = (s32[2,2,8]{2,1,0:T(2,128)S(1)}, s32[2,2,8]{2,1,0:T(2,128)}, u32[]{:S(2)}) copy-start(s32[2,2,8]{2,1,0:T(2,128)} %param.24) | copy-start | bytes 388
  32.0 7.2 %copy-start.6 = (s32[2,2,8]{2,1,0:T(2,128)S(1)}, s32[2,2,8]{2,1,0:T(2,128)}, u32[]{:S(2)}) copy-start(s32[2,2,8]{2,1,0:T(2,128)} %param.23) | copy-start | bytes 388
  32.0 102.6 %copy-start.9 = (bf16[7168,16]{0,1:T(8,128)(2,1)S(1)}, bf16[7168,16]{0,1:T(8,128)(2,1)}, u32[]{:S(2)}) copy-start(bf16[7168,16]{0,1:T(8,128)(2,1)} %param.22) | copy-start | bytes 688132
  160.8 32.6 %copy-start.1 = (bf16[512,512]{1,0:T(8,128)(2,1)S(1)}, bf16[512,512]{1,0:T(8,128)(2,1)}, u32[]{:S(2)}) copy-start(bf16[512,512]{1,0:T(8,128)(2,1)} %param.19) | copy-start | bytes 1572868
Sparse Core Ops, SparseCore 0:
  38.0 95.3 all-reduce.2
where the time goes:
time: 201 us; the launch traced here: 200 us
  waiting for transfers between devices  94.1 us (47%)
  blocking collectives  50.8 us (25%)
  matrix products  35.3 us (18%)
  between operations  14.4 us (7%)
  other arithmetic  3.06 us (2%)
  local copies, waits for them, and re-layouts  2.7 us (1%)
    unnamed x2, waiting for transfers between devices  94.1 us
    all_to_all x1, blocking collectives, body(): lax.all_to_all(outgoing, 'ep', split_axis=1, concat_axis=0, tiled=True)  17.2 us
    all_to_all x1, blocking collectives, body(): lax.all_to_all(produced.astype(jnp.bfloat16), 'ep', split_axis=0, concat_...  16.8 us
    all_to_all x1, blocking collectives, body(): lax.all_to_all(outgoing_rows, 'ep', split_axis=0, concat_axis=0, tiled=True)  16.8 us
    dot_general x1, matrix products, expert_ffn(): return jnp.dot(act, w_down, preferred_element_type=jnp.float32)  14.6 us
    dot_general x1, matrix products, expert_ffn(): gate = jnp.dot(token_rows, w_gate, preferred_element_type=jnp.float32)  7.79 us
    dot_general x1, matrix products, body(): jnp.dot(values, out_proj, preferred_element_type=jnp.float32)  5.78 us
  transfers between devices with their start and end apart: 1, of which 1 were waited for; matrix products, arithmetic and copies ran while one was open for 0% of the time, Pallas kernels for 0%

commit v1 on v0

v1 whole, which is shorter than its diff:
```python
import functools
import math

import jax
import jax.numpy as jnp
from jax import lax
from jax.experimental import pallas as pl
from jax.experimental.pallas import tpu as pltpu
from jax.sharding import PartitionSpec as P

D = 7168
H = 64
LAT = 512
VH = 128
EXPERTS = 16
TOP = 8
CAP = 2
QK = 192


route_scale = 2.827
norm_eps = 1e-06


def softmax_parts(score_cache, score_new):
    row_peak = jnp.maximum(jnp.max(score_cache, axis=-1), jnp.max(score_new, axis=-1))
    exp_cache = jnp.exp(score_cache - row_peak[..., None])
    exp_new = jnp.exp(score_new - row_peak[..., None])
    exp_total = jnp.sum(exp_cache, axis=-1) + jnp.sum(exp_new, axis=-1)
    prob_cache = (exp_cache / exp_total[..., None]).astype(jnp.bfloat16)
    prob_new = (exp_new / exp_total[..., None]).astype(jnp.bfloat16)
    return (prob_cache, prob_new)


def attention(cache_kv, new_kv, queries, lengths):
    score_scale = 1.0 / math.sqrt(QK)
    cache_len = cache_kv.shape[1]
    step_count = new_kv.shape[1]
    score_new = (
        jnp.einsum("bshk,btk->bsht", queries, new_kv, preferred_element_type=jnp.float32)
        * score_scale
    )
    step_ids = jnp.arange(step_count, dtype=jnp.int32)
    causal = step_ids[None, :] <= step_ids[:, None]
    score_new = jnp.where(causal[None, :, None, :], score_new, -jnp.inf)
    score_cache = (
        jnp.einsum("bshk,bpk->bshp", queries, cache_kv, preferred_element_type=jnp.float32)
        * score_scale
    )
    position = jnp.arange(cache_len, dtype=jnp.int32)
    is_live = position[None, :] < lengths[:, None]
    score_cache = jnp.where(is_live[:, None, None, :], score_cache, -jnp.inf)
    prob_cache, prob_new = softmax_parts(score_cache, score_new)
    context = jnp.einsum(
        "bshp,bpc->bshc", prob_cache, cache_kv[:, :, :LAT], preferred_element_type=jnp.float32
    )
    context = context + jnp.einsum(
        "bsht,btc->bshc", prob_new, new_kv[:, :, :LAT], preferred_element_type=jnp.float32
    )
    return context.astype(jnp.bfloat16)


F32 = jnp.float32
BF16 = jnp.bfloat16
CORES = 2
LINE = 4
CHUNKS = 4


def loop(count, step, start=0):
    lax.fori_loop(start, count, lambda i, carry: (step(i), carry)[1], 0)


def layer_kernel(
    n,
    ctx_ref,
    resid_ref,
    gain_ref,
    router_ref,
    ids_ref,
    slots_ref,
    vu_hbm,
    op_hbm,
    wg_hbm,
    wu_hbm,
    wd_hbm,
    out_ref,
    vu,
    op,
    wg,
    wu,
    wd,
    ctx_in,
    rows32,
    acc32,
    gate_acc,
    up_acc,
    hid,
    part,
    pair_sum,
    line_sum,
    in_core0,
    in_mid0,
    in_line0,
    in_core1,
    in_mid1,
    in_line1,
    gathered,
    share_out,
    share_in,
    share_all,
    w_sem,
    ctx_send,
    ctx_recv,
    share_send,
    share_recv,
    core_sem,
    mid_send,
    mid_recv,
    line_send,
    line_recv,
):
    me = lax.axis_index("ep")
    mids = n // (CORES * LINE)
    c = me % CORES
    b = (me // CORES) % mids
    a = me // (CORES * mids)
    toks, width = resid_ref.shape
    part_w = width // CHUNKS
    rows_each = ctx_ref.shape[1]
    heads_per = rows_each // toks
    value_cols = vu.shape[1]
    total = n * toks
    fan = CORES * mids
    per = 8 // toks

    def stack(ref, block, rows):
        group = 8 // rows

        def put(g):
            tile = jnp.concatenate([block(g * group + h) for h in range(group)], axis=0)
            ref[pl.ds(pl.multiple_of(g * 8, 8), 8), :] = tile

        loop(n // group, put)

    def dev(aa, bb, cc):
        return (aa * mids + bb) * CORES + cc

    def send(src, dst, s_sem, r_sem, target):
        return pltpu.make_async_remote_copy(
            src_ref=src,
            dst_ref=dst,
            send_sem=s_sem,
            recv_sem=r_sem,
            device_id={"ep": target},
            device_id_type=pl.DeviceIdType.MESH,
        )

    def cols(ch):
        return pl.ds(pl.multiple_of(ch * part_w, part_w), part_w)

    def op_copy(ch):
        return pltpu.make_async_copy(op_hbm.at[:, cols(ch)], op.at[ch], w_sem.at[0, ch])

    def wg_copy(ch):
        return pltpu.make_async_copy(wg_hbm.at[cols(ch), :], wg.at[ch], w_sem.at[1, ch])

    def wu_copy(ch):
        return pltpu.make_async_copy(wu_hbm.at[cols(ch), :], wu.at[ch], w_sem.at[2, ch])

    def wd_copy(ch):
        return pltpu.make_async_copy(wd_hbm.at[:, cols(ch)], wd.at[ch], w_sem.at[3, ch])

    vu_copy = pltpu.make_async_copy(vu_hbm, vu, w_sem.at[4, 0])
    vu_copy.start()

    barrier = pltpu.get_barrier_semaphore()

    def greet(i):
        pl.semaphore_signal(
            barrier,
            inc=1,
            device_id={"ep": (me + i) % n},
            device_id_type=pl.DeviceIdType.MESH,
        )

    loop(n, greet, 1)
    loop(CHUNKS, lambda ch: op_copy(ch).start())
    pl.semaphore_wait(barrier, n - 1)

    def ctx_copy(i):
        to = (me + i) % n
        return send(ctx_ref.at[to], ctx_in.at[me], ctx_send.at[to], ctx_recv.at[me], to)

    def ctx_arrival(i):
        frm = (me + i) % n
        return send(ctx_ref.at[frm], ctx_in.at[frm], ctx_send.at[frm], ctx_recv.at[frm], frm)

    loop(n, lambda i: ctx_copy(i).start(), 1)

    def start_ffn(ch):
        wg_copy(ch).start()
        wu_copy(ch).start()

    loop(CHUNKS, start_ffn)
    loop(CHUNKS, lambda ch: wd_copy(ch).start())

    lane = lax.broadcasted_iota(jnp.int32, (toks, EXPERTS), 1)
    named = jnp.zeros((toks, EXPERTS), F32)
    kept = jnp.zeros((toks, EXPERTS), F32)
    for k in range(TOP):
        hit = jnp.where(ids_ref[:, k : k + 1] == lane, 1.0, 0.0)
        named = named + hit
        kept = kept + jnp.where(slots_ref[:, k : k + 1] < CAP, hit, 0.0)

    ctx_in[me] = ctx_ref[me]
    vu_copy.wait()
    loop(n, lambda i: ctx_arrival(i).wait_recv(), 1)

    if rows_each % 16 == 0:
        head_rows = ctx_in[...].reshape(n * rows_each, LAT)
    else:

        stack(rows32, lambda i: ctx_in[i].astype(F32), rows_each)
        head_rows = rows32[...].astype(BF16)
    values = jnp.dot(head_rows, vu[...], preferred_element_type=F32)
    if heads_per > 1:
        shape = (n * rows_each, value_cols)
        row_head = lax.broadcasted_iota(jnp.int32, shape, 0) % heads_per
        col_head = lax.broadcasted_iota(jnp.int32, shape, 1) // (value_cols // heads_per)
        values = jnp.where(row_head == col_head, values, 0.0).astype(BF16)
        shape = (total, n * rows_each)
        row_tok = lax.broadcasted_iota(jnp.int32, shape, 1) // heads_per
        fold = jnp.where(row_tok == lax.broadcasted_iota(jnp.int32, shape, 0), 1.0, 0.0)
        values = jnp.dot(fold.astype(BF16), values, preferred_element_type=F32)
    values = values.astype(BF16)

    def reduce_scatter(which, produce, finish):
        in_core, in_mid, in_line = (
            (in_core0, in_mid0, in_line0) if which == 0 else (in_core1, in_mid1, in_line1)
        )

        def core_copy(ch):
            return send(
                part.at[ch, 1 - c],
                in_core.at[ch],
                core_sem.at[which, 0, ch],
                core_sem.at[which, 1, ch],
                dev(a, b, 1 - c),
            )

        def mid_copy(ch, i):
            bb = (b + i) % mids
            return send(
                pair_sum.at[ch, bb],
                in_mid.at[ch, b],
                mid_send.at[which, ch, bb],
                mid_recv.at[which, ch, b],
                dev(a, bb, c),
            )

        def mid_arrival(ch, bb):
            return send(
                pair_sum.at[ch, bb],
                in_mid.at[ch, bb],
                mid_send.at[which, ch, bb],
                mid_recv.at[which, ch, bb],
                dev(a, bb, c),
            )

        def line_copy(ch, i):
            aa = (a + i) % LINE
            return send(
                line_sum.at[ch, aa],
                in_line.at[ch, a],
                line_send.at[which, ch, aa],
                line_recv.at[which, ch, a],
                dev(aa, b, c),
            )

        def line_arrival(ch, aa):
            return send(
                line_sum.at[ch, aa],
                in_line.at[ch, aa],
                line_send.at[which, ch, aa],
                line_recv.at[which, ch, aa],
                dev(aa, b, c),
            )

        def stage1(ch):
            acc32[...] = produce(ch)

            def spread(g):
                tile = acc32[pl.ds(pl.multiple_of(g * 8, 8), 8), :]
                for h in range(per):
                    d = g * per + h
                    part[ch, d % CORES, (d // CORES) % mids, d // fan] = tile[
                        h * toks : (h + 1) * toks
                    ].astype(BF16)

            loop(n // per, spread)
            core_copy(ch).start()

        def stage2(ch):
            core_copy(ch).wait_recv()

            def add_pair(k):
                bb, aa = k // LINE, k % LINE
                pair_sum[ch, bb, aa] = (
                    part[ch, c, bb, aa].astype(F32) + in_core[ch, bb, aa].astype(F32)
                ).astype(BF16)

            loop(mids * LINE, add_pair)
            loop(mids, lambda i: mid_copy(ch, i).start(), 1)

        def stage3(ch):
            loop(mids, lambda i: mid_arrival(ch, (b + i) % mids).wait_recv(), 1)

            def add_mid(aa):
                acc = pair_sum[ch, b, aa].astype(F32)
                acc = lax.fori_loop(
                    1, mids, lambda i, t: t + in_mid[ch, (b + i) % mids, aa].astype(F32), acc
                )
                line_sum[ch, aa] = acc.astype(BF16)

            loop(LINE, add_mid)
            loop(LINE, lambda i: line_copy(ch, i).start(), 1)

        def stage4(ch):
            acc = line_sum[ch, a].astype(F32)
            for i in range(1, LINE):
                aa = (a + i) % LINE
                line_arrival(ch, aa).wait_recv()
                acc = acc + in_line[ch, aa].astype(F32)
            finish(ch, acc)

        def step(t):
            for delay, stage in enumerate((stage1, stage2, stage3, stage4)):
                pl.when((t >= delay) & (t < CHUNKS + delay))(
                    functools.partial(stage, t - delay)
                )

        loop(CHUNKS + 3, step)

        def drain(ch):
            core_copy(ch).wait_send()
            loop(mids, lambda i: mid_copy(ch, i).wait_send(), 1)
            loop(LINE, lambda i: line_copy(ch, i).wait_send(), 1)

        loop(CHUNKS, drain)

    def attended_part(ch):
        op_copy(ch).wait()
        return jnp.dot(values, op[ch], preferred_element_type=F32)

    def keep_hidden(ch, acc):
        hid[ch] = acc + resid_ref[:, cols(ch)].astype(F32)

    reduce_scatter(0, attended_part, keep_hidden)

    square = jnp.zeros((toks, 1), F32)
    for ch in range(CHUNKS):
        square = square + jnp.sum(hid[ch] * hid[ch], axis=-1, keepdims=True)
    scale = lax.rsqrt(square / width + norm_eps)

    def leg_line(ch, i):
        aa = (a + i) % LINE
        blk = gathered.at[ch, c, b, a]
        return send(blk, blk, line_send.at[2, ch, aa], line_recv.at[2, ch, a], dev(aa, b, c))

    def leg_line_arrival(ch, aa):
        blk = gathered.at[ch, c, b, aa]
        return send(blk, blk, line_send.at[2, ch, aa], line_recv.at[2, ch, aa], dev(aa, b, c))

    def leg_mid(ch, i):
        bb = (b + i) % mids
        blk = gathered.at[ch, c, b]
        return send(blk, blk, mid_send.at[2, ch, bb], mid_recv.at[2, ch, b], dev(a, bb, c))

    def leg_mid_arrival(ch, bb):
        blk = gathered.at[ch, c, bb]
        return send(blk, blk, mid_send.at[2, ch, bb], mid_recv.at[2, ch, bb], dev(a, bb, c))

    def leg_core(ch):
        blk = gathered.at[ch, c]
        return send(
            blk, blk, core_sem.at[2, 0, ch], core_sem.at[2, 1, ch], dev(a, b, 1 - c)
        )

    def leg_core_arrival(ch):
        blk = gathered.at[ch, 1 - c]
        return send(
            blk, blk, core_sem.at[2, 0, ch], core_sem.at[2, 1, ch], dev(a, b, 1 - c)
        )

    logits = jnp.zeros((toks, EXPERTS), F32)
    for ch in range(CHUNKS):
        span = slice(ch * part_w, (ch + 1) * part_w)
        normed = (hid[ch] * scale * gain_ref[:, span].astype(F32)).astype(BF16)
        gathered[ch, c, b, a] = normed
        for i in range(1, LINE):
            leg_line(ch, i).start()
        logits = logits + lax.dot_general(
            normed,
            router_ref[:, span],
            (((1,), (1,)), ((), ())),
            preferred_element_type=F32,
        )
    gates = jax.nn.sigmoid(logits)
    shares = route_scale * gates / jnp.sum(gates * named, axis=1, keepdims=True) * kept
    share_out[...] = jnp.zeros_like(share_out)
    share_out[:, :EXPERTS] = shares

    def share_copy(i):
        to = (me + i) % n
        return send(share_out, share_in.at[me], share_send.at[to], share_recv.at[me], to)

    def share_arrival(i):
        frm = (me + i) % n
        return send(share_out, share_in.at[frm], share_send.at[frm], share_recv.at[frm], frm)

    gate_acc[...] = jnp.zeros_like(gate_acc)
    up_acc[...] = jnp.zeros_like(up_acc)

    def hop_mid(ch):
        for i in range(1, LINE):
            leg_line_arrival(ch, (a + i) % LINE).wait_recv()
        loop(mids, lambda i: leg_mid(ch, i).start(), 1)

    def hop_core(ch):
        loop(mids, lambda i: leg_mid_arrival(ch, (b + i) % mids).wait_recv(), 1)
        leg_core(ch).start()

    def multiply(ch):
        leg_core_arrival(ch).wait_recv()

        def block(d):
            return gathered[ch, d % CORES, (d // CORES) % mids, d // fan].astype(F32)

        stack(acc32, block, toks)
        x = acc32[...].astype(BF16)
        wg_copy(ch).wait()
        gate_acc[...] += jnp.dot(x, wg[ch], preferred_element_type=F32)
        wu_copy(ch).wait()
        up_acc[...] += jnp.dot(x, wu[ch], preferred_element_type=F32)

    def gather_step(t):
        for delay, stage in enumerate((hop_mid, hop_core, multiply)):
            pl.when((t >= delay) & (t < CHUNKS + delay))(functools.partial(stage, t - delay))

    loop(n, lambda i: share_copy(i).start(), 1)
    loop(CHUNKS + 2, gather_step)

    share_in[me] = share_out[...]
    loop(n, lambda i: share_arrival(i).wait_recv(), 1)

    stack(share_all, lambda d: share_in[d], toks)
    mine = lax.broadcasted_iota(jnp.int32, share_all.shape, 1) == me // (n // EXPERTS)
    share = jnp.sum(jnp.where(mine, share_all[...], 0.0), axis=1, keepdims=True)
    gate = gate_acc[...]
    act = (gate * jax.nn.sigmoid(gate) * up_acc[...]).astype(BF16)

    def expert_part(ch):
        wd_copy(ch).wait()
        return jnp.dot(act, wd[ch], preferred_element_type=F32) * share

    def put_out(ch, acc):
        out_ref[:, cols(ch)] = (hid[ch] + acc).astype(BF16)

    reduce_scatter(1, expert_part, put_out)

    def drain_pairs(i):
        ctx_copy(i).wait_send()
        share_copy(i).wait_send()

    loop(n, drain_pairs, 1)

    def drain_gather(ch):
        for i in range(1, LINE):
            leg_line(ch, i).wait_send()
        loop(mids, lambda i: leg_mid(ch, i).wait_send(), 1)
        leg_core(ch).wait_send()

    loop(CHUNKS, drain_gather)


def body(
    cache_kv,
    new_kv,
    queries,
    lengths,
    resid,
    value_up,
    out_proj,
    norm_gain,
    router,
    expert_ids,
    slots,
    w_gate,
    w_up,
    w_down,
):
    n = lax.axis_size("ep")
    context = attention(cache_kv, new_kv, queries, lengths)
    toks = context.shape[0] * context.shape[1]
    heads = context.shape[2]
    width = resid.shape[-1]
    context = context.reshape(toks, heads, LAT)
    value_cols = value_up.shape[1]
    heads_per = max(1, value_cols // VH)
    if value_cols < VH:
        context = jnp.repeat(context, VH // value_cols, axis=1)
    outgoing = context.reshape(toks, n, heads_per, LAT).transpose(1, 0, 2, 3)
    outgoing = outgoing.reshape(n, toks * heads_per, LAT)
    hidden_units = w_gate.shape[1]
    mids = n // (CORES * LINE)
    part_w = width // CHUNKS
    total = n * toks
    vmem = pl.BlockSpec(memory_space=pltpu.VMEM)
    hbm = pl.BlockSpec(memory_space=pl.ANY)
    landing = [
        pltpu.VMEM((CHUNKS, mids, LINE, toks, part_w), BF16),
        pltpu.VMEM((CHUNKS, mids, LINE, toks, part_w), BF16),
        pltpu.VMEM((CHUNKS, LINE, toks, part_w), BF16),
    ]
    dma = pltpu.SemaphoreType.DMA
    mixed = pl.pallas_call(
        functools.partial(layer_kernel, n),
        out_shape=jax.ShapeDtypeStruct((toks, width), BF16),
        in_specs=[vmem] * 6 + [hbm] * 5,
        out_specs=vmem,
        scratch_shapes=[
            pltpu.VMEM(value_up.shape, BF16),
            pltpu.VMEM((CHUNKS, out_proj.shape[0], part_w), BF16),
            pltpu.VMEM((CHUNKS, part_w, hidden_units), BF16),
            pltpu.VMEM((CHUNKS, part_w, hidden_units), BF16),
            pltpu.VMEM((CHUNKS, hidden_units, part_w), BF16),
            pltpu.VMEM(outgoing.shape, BF16),
            pltpu.VMEM((n * toks * heads_per if toks * heads_per % 16 else 8, LAT), F32),
            pltpu.VMEM((total, part_w), F32),
            pltpu.VMEM((total, hidden_units), F32),
            pltpu.VMEM((total, hidden_units), F32),
            pltpu.VMEM((CHUNKS, toks, part_w), F32),
            pltpu.VMEM((CHUNKS, CORES, mids, LINE, toks, part_w), BF16),
            pltpu.VMEM((CHUNKS, mids, LINE, toks, part_w), BF16),
            pltpu.VMEM((CHUNKS, LINE, toks, part_w), BF16),
            *landing,
            *landing,
            pltpu.VMEM((CHUNKS, CORES, mids, LINE, toks, part_w), BF16),
            pltpu.VMEM((toks, 128), F32),
            pltpu.VMEM((n, toks, 128), F32),
            pltpu.VMEM((total, 128), F32),
            dma((5, CHUNKS)),
            dma((n,)),
            dma((n,)),
            dma((n,)),
            dma((n,)),
            dma((3, 2, CHUNKS)),
            dma((3, CHUNKS, mids)),
            dma((3, CHUNKS, mids)),
            dma((3, CHUNKS, LINE)),
            dma((3, CHUNKS, LINE)),
        ],
        compiler_params=pltpu.CompilerParams(
            collective_id=0, has_side_effects=True, vmem_limit_bytes=67043328
        ),
    )(
        outgoing,
        resid.reshape(toks, width),
        norm_gain.reshape(1, width),
        router.T,
        expert_ids.reshape(toks, TOP),
        slots.reshape(toks, TOP),
        value_up,
        out_proj,
        w_gate,
        w_up,
        w_down,
    )
    return mixed.reshape(resid.shape)


def solution(mesh):
    return jax.shard_map(
        body,
        mesh=mesh,
        in_specs=(
            P(("rep", "ep"), None, None),
            P(("rep", "ep"), None, None),
            P(("rep", "ep"), None, None, None),
            P(("rep", "ep")),
            P(("rep", "ep"), None, None),
            P(None, "ep"),
            P("ep", None),
            P(),
            P(),
            P(("rep", "ep"), None, None),
            P(("rep", "ep"), None, None),
            P(None, "ep"),
            P(None, "ep"),
            P("ep", None),
        ),
        out_specs=P(("rep", "ep"), None, None),
        check_vma=False,
    )
```

time: 201 us -> 80.7 us (0.40)
  waiting for transfers between devices: 94.1 us -> 0 us
  Pallas kernels: 0 us -> 69 us
  blocking collectives: 50.8 us -> 0 us
  matrix products: 35.3 us -> 6.3 us
  between operations: 14.4 us -> 0.14 us
    unnamed x2 -> x0, waiting for transfers between devices: 94.1 us -> none
    pallas_call x0 -> x1, Pallas kernels: none -> 69 us  [body(): pl.pallas_call(functools.partial(layer_kernel, n), out_shape=jax.ShapeDty...]
    all_to_all x3 -> x0, blocking collectives: 50.8 us -> none  [the longest x1 17.2 us: body(): lax.all_to_all(outgoing, 'ep', split_axis=1, concat_axis=0, tiled=True)]
    dot_general x7 -> x0, matrix products: 29.3 us -> none  [the longest x1 14.6 us: expert_ffn(): return jnp.dot(act, w_down, preferred_element_type=jnp.float32)]
  transfers between devices with their start and end apart: 1 -> 0, of which waited for: 1 -> 0; matrix products, arithmetic and copies ran while one was open for 0% -> 0% of each run, Pallas kernels for 0% -> 0%
where the time goes in v1:
time: 80.7 us; the launch traced here: 80.5 us
  Pallas kernels  69 us (86%)
  matrix products  6.3 us (8%)
  local copies, waits for them, and re-layouts  3.73 us (5%)
  other arithmetic  1.36 us (2%)
    pallas_call x1, Pallas kernels, body(): pl.pallas_call(functools.partial(layer_kernel, n), out_shape=jax.ShapeDty...  69 us
    dot_general x1, matrix products, attention(): jnp.einsum('bshk,bpk->bshp', queries, cache_kv, preferred_element_type=jn...  4.02 us
    dot_general x1, matrix products, attention(): jnp.einsum('bshp,bpc->bshc', prob_cache, cache_kv[:, :, :LAT], preferred_...  1.72 us

profile of v1, /device:TPU:0, one launch (start us, length us, event | category | flops | bytes accessed | tf_op | source)
XLA Modules:
  0.0 80.5 jit_solution(7811210357631179403)
XLA Ops:
  0.0 0.0 slice-start
  0.0 0.9 %iota_compare_fusion = pred[2,2048]{1,0:T(4,128)(4,1)S(1)} fusion(s32[2]{0:T(128)} %param.17), kind=kLoop, calls=%fused_computation.17 | loop fusion | flops 4096 | bytes 4104 | tf_op jit(solution)/shard_map/lt | solution.py:51
  0.9 0.0 copy-start
  0.9 0.0 copy-start.3
  0.9 0.0 slice-start.1
  0.9 4.0 %fusion.22 = (f32[2,2,64]{2,1,0:T(2,128)S(1)}, f32[2,2,64,2048]{3,2,1,0:T(8,128)S(1)}) fusion(bf16[2,2,64,576]{3,2,1,0:T(8,128)(2,1)} %param.16, bf16[2,2048,576]{1,2,0:T(8,128)(2,1)} %param.14, pred[2,2048]{1,0:T(4,128)(4,1)S(1)} %iota_compare_fusion), kind=kOutput, calls=%fused_computation.27 | convolution fusion | flops 605552384 | bytes 7115776 | tf_op jit(solution)/shard_map/bshk,bpk->bshp/dot_general | solution.py:47
  5.0 0.0 copy-done
  5.0 0.0 copy-done.3
  5.0 0.3 fusion.23
  5.3 0.4 fusion.11
  5.8 0.0 slice-done
  5.8 0.0 slice-done.1
  5.8 1.7 %fusion.2 = f32[2,2,64,512]{3,2,1,0:T(8,128)S(1)} fusion(bf16[2,2048,576]{1,2,0:T(8,128)(2,1)S(1)} %bitcast.40, f32[2,2,64,2048]{3,2,1,0:T(8,128)S(1)} %get-tuple-element.6, f32[2,2,64]{2,1,0:T(2,128)S(1)} %add.10, f32[2,2,64]{2,1,0:T(2,128)S(1)} %max.7), kind=kOutput, calls=%fused_computation.2 | convolution fusion | flops 538443776 | bytes 6819840 | tf_op jit(solution)/shard_map/bshp,bpc->bshc/dot_general | solution.py:54
  7.5 0.0 copy-start.1
  7.5 0.0 copy-start.2
  7.5 0.3 fusion.12
  7.8 0.1 reshape_reshape.3
  7.9 0.1 copy.23
  8.0 0.8 reshape.57.ctx_ref
  8.8 0.0 copy-done.1
  8.8 0.7 reshape.58.resid_ref
  9.4 0.0 copy-done.2
  9.4 0.6 reshape.59.gain_ref
  10.1 69.0 %shard_map.136 = bf16[4,7168]{1,0:T(4,128)(2,1)} custom-call(bf16[16,16,512]{2,1,0:T(8,128)(2,1)} %reshape.57.ctx_ref, bf16[4,7168]{1,0:T(4,128)(2,1)} %reshape.58.resid_ref, bf16[1,7168]{1,0:T(2,128)(2,1)} %reshape.59.gain_ref, bf16[16,7168]{1,0:T(8,128)(2,1)} %bitcast.42, s32[4,8]{1,0:T(4,128)} %bitcast.43, s32[4,8]{1,0:T(4,128)} %bitcast.44, ...), custom_call_target="tpu_custom_call" | custom-call | tf_op jit(solution)/shard_map/pallas_call | solution.py:527
  79.1 1.5 %reshape.62 = bf16[2,2,7168]{2,1,0:T(2,128)(2,1)} reshape(bf16[4,7168]{1,0:T(4,128)(2,1)} %shard_map.136) | data formatting | bytes 114688 | tf_op jit(solution)/shard_map/reshape | solution.py:580
  (5 shorter events, 0.0 us)
Async XLA Ops:
  0.0 5.8 %slice-start = ((s8[4718592]{0:T(1024)(128)(4,1)}), s8[4194304]{0:T(1024)(128)(4,1)S(1)}, s32[]{:S(2)}) async-start(s8[4718592]{0:T(1024)(128)(4,1)} %bitcast.39), calls=%async_computation | async-start | bytes 8388608
  0.9 4.1 %copy-start = (bf16[2,2,64,576]{3,2,1,0:T(8,128)(2,1)S(1)}, bf16[2,2,64,576]{3,2,1,0:T(8,128)(2,1)}, u32[]{:S(2)}) copy-start(bf16[2,2,64,576]{3,2,1,0:T(8,128)(2,1)} %param.16) | copy-start | bytes 884740
  0.9 4.1 %copy-start.3 = (bf16[2,2,576]{2,1,0:T(2,128)(2,1)S(1)}, bf16[2,2,576]{2,1,0:T(2,128)(2,1)}, u32[]{:S(2)}) copy-start(bf16[2,2,576]{2,1,0:T(2,128)(2,1)} %param.15) | copy-start | bytes 13828
  0.9 4.8 %slice-start.1 = ((s8[4718592]{0:T(1024)(128)(4,1)}), s8[524288]{0:T(1024)(128)(4,1)S(1)}, s32[]{:S(2)}) async-start(s8[4718592]{0:T(1024)(128)(4,1)} %bitcast.39), calls=%async_computation.1 | async-start | bytes 1048576
  7.5 1.3 %copy-start.1 = (bf16[2,2,7168]{2,1,0:T(2,128)(2,1)S(1)}, bf16[2,2,7168]{2,1,0:T(2,128)(2,1)}, u32[]{:S(2)}) copy-start(bf16[2,2,7168]{2,1,0:T(2,128)(2,1)} %param.18) | copy-start | bytes 172036
  7.5 1.9 %copy-start.2 = (bf16[7168]{0:T(1024)(128)(2,1)S(1)}, bf16[7168]{0:T(1024)(128)(2,1)}, u32[]{:S(2)}) copy-start(bf16[7168]{0:T(1024)(128)(2,1)} %param.21) | copy-start | bytes 43012

commit v2 on v1

--- a/solution.py
+++ b/solution.py
@@ -22,44 +22,6 @@
 norm_eps = 1e-06
 
 
-def softmax_parts(score_cache, score_new):
-    row_peak = jnp.maximum(jnp.max(score_cache, axis=-1), jnp.max(score_new, axis=-1))
-    exp_cache = jnp.exp(score_cache - row_peak[..., None])
-    exp_new = jnp.exp(score_new - row_peak[..., None])
-    exp_total = jnp.sum(exp_cache, axis=-1) + jnp.sum(exp_new, axis=-1)
-    prob_cache = (exp_cache / exp_total[..., None]).astype(jnp.bfloat16)
-    prob_new = (exp_new / exp_total[..., None]).astype(jnp.bfloat16)
-    return (prob_cache, prob_new)
-
-
-def attention(cache_kv, new_kv, queries, lengths):
-    score_scale = 1.0 / math.sqrt(QK)
-    cache_len = cache_kv.shape[1]
-    step_count = new_kv.shape[1]
-    score_new = (
-        jnp.einsum("bshk,btk->bsht", queries, new_kv, preferred_element_type=jnp.float32)
-        * score_scale
-    )
-    step_ids = jnp.arange(step_count, dtype=jnp.int32)
-    causal = step_ids[None, :] <= step_ids[:, None]
-    score_new = jnp.where(causal[None, :, None, :], score_new, -jnp.inf)
-    score_cache = (
-        jnp.einsum("bshk,bpk->bshp", queries, cache_kv, preferred_element_type=jnp.float32)
-        * score_scale
-    )
-    position = jnp.arange(cache_len, dtype=jnp.int32)
-    is_live = position[None, :] < lengths[:, None]
-    score_cache = jnp.where(is_live[:, None, None, :], score_cache, -jnp.inf)
-    prob_cache, prob_new = softmax_parts(score_cache, score_new)
-    context = jnp.einsum(
-        "bshp,bpc->bshc", prob_cache, cache_kv[:, :, :LAT], preferred_element_type=jnp.float32
-    )
-    context = context + jnp.einsum(
-        "bsht,btc->bshc", prob_new, new_kv[:, :, :LAT], preferred_element_type=jnp.float32
-    )
-    return context.astype(jnp.bfloat16)
-
-
 F32 = jnp.float32
 BF16 = jnp.bfloat16
 CORES = 2
@@ -73,12 +35,15 @@
 
 def layer_kernel(
     n,
-    ctx_ref,
-    resid_ref,
+    len_ref,
+    new_ref,
     gain_ref,
     router_ref,
     ids_ref,
     slots_ref,
+    cache_hbm,
+    query_hbm,
+    resid_hbm,
     vu_hbm,
     op_hbm,
     wg_hbm,
@@ -90,6 +55,12 @@
     wg,
     wu,
     wd,
+    keys,
+    fresh,
+    query,
+    resid,
+    ctx32,
+    ctx_ref,
     ctx_in,
     rows32,
     acc32,
@@ -110,6 +81,7 @@
     share_in,
     share_all,
     w_sem,
+    key_sem,
     ctx_send,
     ctx_recv,
     share_send,
@@ -125,7 +97,8 @@
     c = me % CORES
     b = (me // CORES) % mids
     a = me // (CORES * mids)
-    toks, width = resid_ref.shape
+    seqs, steps, width = resid.shape
+    toks = seqs * steps
     part_w = width // CHUNKS
     rows_each = ctx_ref.shape[1]
     heads_per = rows_each // toks
@@ -172,7 +145,20 @@
         return pltpu.make_async_copy(wd_hbm.at[:, cols(ch)], wd.at[ch], w_sem.at[3, ch])
 
     vu_copy = pltpu.make_async_copy(vu_hbm, vu, w_sem.at[4, 0])
+    resid_copy = pltpu.make_async_copy(resid_hbm, resid, w_sem.at[4, 1])
+    cache_len = cache_hbm.shape[2]
+
+    def key_copy(q):
+        return pltpu.make_async_copy(cache_hbm.at[q], keys.at[q], key_sem.at[0, q])
+
+    def query_copy(q):
+        return pltpu.make_async_copy(query_hbm.at[q], query.at[q], key_sem.at[1, q])
+
+    for q in range(seqs):
+        query_copy(q).start()
+        key_copy(q).start()
     vu_copy.start()
+    resid_copy.start()
 
     barrier = pltpu.get_barrier_semaphore()
 
@@ -186,6 +172,57 @@
 
     loop(n, greet, 1)
     loop(CHUNKS, lambda ch: op_copy(ch).start())
+
+    def start_ffn(ch):
+        wg_copy(ch).start()
+        wu_copy(ch).start()
+
+    loop(CHUNKS, start_ffn)
+    loop(CHUNKS, lambda ch: wd_copy(ch).start())
+
+    rows_q, span_new = query.shape[1], fresh.shape[1]
+    heads = rows_q // steps
+    score_scale = 1.0 / math.sqrt(QK)
+    fresh[...] = jnp.zeros_like(fresh)
+    for q in range(seqs):
+        fresh[q, :steps, :] = new_ref[q]
+    place = lax.broadcasted_iota(jnp.int32, (rows_q, cache_len), 1)
+    newer = lax.broadcasted_iota(jnp.int32, (rows_q, span_new), 1) <= (
+        lax.broadcasted_iota(jnp.int32, (rows_q, span_new), 0) // heads
+    )
+    for q in range(seqs):
+        query_copy(q).wait()
+        key_copy(q).wait()
+        old = jnp.dot(query[q], keys[q], preferred_element_type=F32) * score_scale
+        old = jnp.where(place < len_ref[q], old, -jnp.inf)
+        new = lax.dot_general(
+            query[q], fresh[q], (((1,), (1,)), ((), ())), preferred_element_type=F32
+        )
+        new = jnp.where(newer, new * score_scale, -jnp.inf)
+        peak = jnp.maximum(
+            jnp.max(old, axis=-1, keepdims=True), jnp.max(new, axis=-1, keepdims=True)
+        )
+        old = jnp.exp(old - peak)
+        new = jnp.exp(new - peak)
+        inverse = 1.0 / (
+            jnp.sum(old, axis=-1, keepdims=True) + jnp.sum(new, axis=-1, keepdims=True)
+        )
+        ctx32[q] = lax.dot_general(
+            (old * inverse).astype(BF16),
+            keys[q, :LAT, :],
+            (((1,), (1,)), ((), ())),
+            preferred_element_type=F32,
+        ) + jnp.dot(
+            (new * inverse).astype(BF16), fresh[q, :, :LAT], preferred_element_type=F32
+        )
+    for j in range(n):
+        first = (j * value_cols) // VH
+        rows = [
+            ctx32[q, t * heads + first : t * heads + first + heads_per, :]
+            for q in range(seqs)
+            for t in range(steps)
+        ]
+        ctx_ref[j] = jnp.concatenate(rows, axis=0).astype(BF16)
     pl.semaphore_wait(barrier, n - 1)
 
     def ctx_copy(i):
@@ -197,13 +234,6 @@
         return send(ctx_ref.at[frm], ctx_in.at[frm], ctx_send.at[frm], ctx_recv.at[frm], frm)
 
     loop(n, lambda i: ctx_copy(i).start(), 1)
-
-    def start_ffn(ch):
-        wg_copy(ch).start()
-        wu_copy(ch).start()
-
-    loop(CHUNKS, start_ffn)
-    loop(CHUNKS, lambda ch: wd_copy(ch).start())
 
     lane = lax.broadcasted_iota(jnp.int32, (toks, EXPERTS), 1)
     named = jnp.zeros((toks, EXPERTS), F32)
@@ -354,8 +384,10 @@
         return jnp.dot(values, op[ch], preferred_element_type=F32)
 
     def keep_hidden(ch, acc):
-        hid[ch] = acc + resid_ref[:, cols(ch)].astype(F32)
-
+        rows = [resid[q, :, cols(ch)].astype(F32) for q in range(seqs)]
+        hid[ch] = acc + jnp.concatenate(rows, axis=0)
+
+    resid_copy.wait()
     reduce_scatter(0, attended_part, keep_hidden)
 
     square = jnp.zeros((toks, 1), F32)
@@ -465,7 +497,9 @@
         return jnp.dot(act, wd[ch], preferred_element_type=F32) * share
 
     def put_out(ch, acc):
-        out_ref[:, cols(ch)] = (hid[ch] + acc).astype(BF16)
+        mixed = hid[ch] + acc
+        for q in range(seqs):
+            out_ref[q, :, cols(ch)] = mixed[q * steps : (q + 1) * steps].astype(BF16)
 
     reduce_scatter(1, expert_part, put_out)
 
@@ -501,17 +535,11 @@
     w_down,
 ):
     n = lax.axis_size("ep")
-    context = attention(cache_kv, new_kv, queries, lengths)
-    toks = context.shape[0] * context.shape[1]
-    heads = context.shape[2]
+    seqs, steps, heads, kv = queries.shape
+    toks = seqs * steps
     width = resid.shape[-1]
-    context = context.reshape(toks, heads, LAT)
-    value_cols = value_up.shape[1]
-    heads_per = max(1, value_cols // VH)
-    if value_cols < VH:
-        context = jnp.repeat(context, VH // value_cols, axis=1)
-    outgoing = context.reshape(toks, n, heads_per, LAT).transpose(1, 0, 2, 3)
-    outgoing = outgoing.reshape(n, toks * heads_per, LAT)
+    heads_per = max(1, value_up.shape[1] // VH)
+    packets = (n, toks * heads_per, LAT)
     hidden_units = w_gate.shape[1]
     mids = n // (CORES * LINE)
     part_w = width // CHUNKS
@@ -526,8 +554,8 @@
     dma = pltpu.SemaphoreType.DMA
     mixed = pl.pallas_call(
         functools.partial(layer_kernel, n),
-        out_shape=jax.ShapeDtypeStruct((toks, width), BF16),
-        in_specs=[vmem] * 6 + [hbm] * 5,
+        out_shape=jax.ShapeDtypeStruct(resid.shape, BF16),
+        in_specs=[pl.BlockSpec(memory_space=pltpu.SMEM)] + [vmem] * 5 + [hbm] * 8,
         out_specs=vmem,
         scratch_shapes=[
             pltpu.VMEM(value_up.shape, BF16),
@@ -535,7 +563,13 @@
             pltpu.VMEM((CHUNKS, part_w, hidden_units), BF16),
             pltpu.VMEM((CHUNKS, part_w, hidden_units), BF16),
             pltpu.VMEM((CHUNKS, hidden_units, part_w), BF16),
-            pltpu.VMEM(outgoing.shape, BF16),
+            pltpu.VMEM((seqs, kv, cache_kv.shape[1]), BF16),
+            pltpu.VMEM((seqs, 128, kv), BF16),
+            pltpu.VMEM((seqs, steps * heads, kv), BF16),
+            pltpu.VMEM(resid.shape, BF16),
+            pltpu.VMEM((seqs, steps * heads, LAT), F32),
+            pltpu.VMEM(packets, BF16),
+            pltpu.VMEM(packets, BF16),
             pltpu.VMEM((n * toks * heads_per if toks * heads_per % 16 else 8, LAT), F32),
             pltpu.VMEM((total, part_w), F32),
             pltpu.VMEM((total, hidden_units), F32),
@@ -551,6 +585,7 @@
             pltpu.VMEM((n, toks, 128), F32),
             pltpu.VMEM((total, 128), F32),
             dma((5, CHUNKS)),
+            dma((2, seqs)),
             dma((n,)),
             dma((n,)),
             dma((n,)),
@@ -565,19 +600,22 @@
             collective_id=0, has_side_effects=True, vmem_limit_bytes=67043328
         ),
     )(
-        outgoing,
-        resid.reshape(toks, width),
+        lengths,
+        new_kv,
         norm_gain.reshape(1, width),
         router.T,
         expert_ids.reshape(toks, TOP),
         slots.reshape(toks, TOP),
+        cache_kv.transpose(0, 2, 1),
+        queries.reshape(seqs, steps * heads, kv),
+        resid,
         value_up,
         out_proj,
         w_gate,
         w_up,
         w_down,
     )
-    return mixed.reshape(resid.shape)
+    return mixed
 
 
 def solution(mesh):

time: 80.7 us -> 76 us (0.942)
  matrix products: 6.3 us -> 0 us
  Pallas kernels: 69 us -> 72.9 us
  other arithmetic: 1.36 us -> 0 us
  local copies, waits for them, and re-layouts: 3.73 us -> 2.82 us
    dot_general x4 -> x0, matrix products: 6.3 us -> none  [the longest x1 4.02 us: attention(): jnp.einsum('bshk,bpk->bshp', queries, cache_kv, preferred_element_type=jn...]
    pallas_call x1, Pallas kernels: 69 us -> 72.9 us  [body(): pl.pallas_call(functools.partial(layer_kernel, n), out_shape=jax.ShapeDty...]
    reshape x3 -> x0, local copies, waits for them, and re-layouts: 2.88 us -> none  [the longest x1 1.47 us: body(): return mixed.reshape(resid.shape)]
    unnamed x12 -> x1, local copies, waits for them, and re-layouts: 0.04 us -> 1.48 us
    lt x1 -> x0, other arithmetic: 0.88 us -> none  [attention(): is_live = position[None, :] < lengths[:, None]]
where the time goes in v2:
time: 76 us; the launch traced here: 75.7 us
  Pallas kernels  72.9 us (96%)
  local copies, waits for them, and re-layouts  2.82 us (4%)
    pallas_call x1, Pallas kernels, body(): pl.pallas_call(functools.partial(layer_kernel, n), out_shape=jax.ShapeDty...  72.9 us

profile of v2, /device:TPU:0, one launch (start us, length us, event | category | flops | bytes accessed | tf_op | source)
XLA Modules:
  0.0 75.7 jit_solution(13593303860467730593)
XLA Ops:
  0.0 1.3 %reshape.12.gain_ref = bf16[1,7168]{1,0:T(2,128)(2,1)} reshape(bf16[7168]{0:T(1024)(128)(2,1)} %param.21) | data formatting | bytes 28672 | tf_op jit(solution)/shard_map/reshape | solution.py:605
  1.3 72.9 %shard_map.136 = bf16[2,2,7168]{2,1,0:T(2,128)(2,1)} custom-call(s32[2]{0:T(128)} %len_ref.1, bf16[2,2,576]{2,1,0:T(2,128)(2,1)} %new_ref.1, bf16[1,7168]{1,0:T(2,128)(2,1)} %reshape.12.gain_ref, bf16[16,7168]{1,0:T(8,128)(2,1)} %bitcast.7, s32[4,8]{1,0:T(4,128)} %bitcast.8, s32[4,8]{1,0:T(4,128)} %bitcast.9, bf16[2,576,2048]{2,1,0:T(8,128)(2,1)} %bitcast.5, ...), custom_call_target="tpu_custom_call" | custom-call | tf_op jit(solution)/shard_map/pallas_call | solution.py:555
  74.3 1.5 %copy.16 = bf16[2,2,7168]{2,1,0:T(2,128)(2,1)} copy(bf16[2,2,7168]{2,1,0:T(2,128)(2,1)} %shard_map.136) | data formatting | bytes 114688
